TPU v7x, 32 devices: a whole 2x2x4 slice. The times are simulated.
32 devices in a mesh: depth: 8 (over z, x), tile: 4 (over y, core).
Axes of the slice: x: 2, y: 2, z: 4, core: 2. Of those that a mesh axis runs over, the one named last changes fastest.
Arguments:
- volume: bfloat16 [64, 256, 4096], P('depth', 'tile'), may hold values from -6 to 6
- shear: int32 [64], replicated, may hold values from -64 to 64, as said below
- footprint: int32 [8, 2], P('depth'), may hold values from 0 to 4096, as said below
Outputs:
- frame: float32 [4, 256, 4096], P(None, 'tile', 'depth')
Inputs may be any that keep to these rules, and one draw needn't show every extreme that they name: Offsets follow a linear tilt over the slices with small jitter; shear[0] and shear[63] are the two ends of the range, in either order. footprint[b, 0] < 1024 and footprint[b, 1] > 3072 for every brick.
All inputs are finite; a program needn't handle non-finite values.
Results may differ from a plain program's by a relative error of at most 0.00085.
Values may be sent and summed in bfloat16 or wider, within the bound.
No kernel may reach another device: no remote copies, remote signals or barrier semaphores. Data moves between devices by JAX's collectives and lax.ppermute only.
A program may use at most 64 MiB of HBM per device.

v0:
```python
import jax
import jax.numpy as jnp
from jax import lax
from jax.sharding import PartitionSpec as P

NY = 4096
SMAX = 64


def extended_2(x, sides, width):
    for axis, dim in sides:
        count, length = (lax.axis_size(axis), x.shape[dim])
        up = [(i, (i + 1) % count) for i in range(count - 1)]
        down = [(j, i) for i, j in up]
        last = lax.slice_in_dim(x, length - width, length, axis=dim)
        leading = lax.slice_in_dim(x, 0, width, axis=dim)
        before = lax.ppermute(last, axis, up)
        after = lax.ppermute(leading, axis, down)
        x = jnp.concatenate([before, x, after], axis=dim)
    return x


def colour(cur, gx, gy, gz, offset, low, high, absorb):
    norm = jnp.sqrt(gx * gx + gy * gy + gz * gz + 1.0)
    shade = 0.3 + 0.7 * jnp.abs(0.48 * gx + 0.6 * gy + 0.64 * gz) / norm
    alpha = 1.0 - jnp.exp(-absorb * cur * cur)
    rgba = jnp.stack(
        [
            shade * jax.nn.sigmoid(1.2 * cur + 0.2) * alpha,
            shade * jax.nn.sigmoid(-0.8 * cur) * alpha,
            shade * jax.nn.sigmoid(0.5 * cur - 0.3) * alpha,
            alpha,
        ]
    )
    padded = jnp.pad(rgba, ((0, 0), (0, 0), (SMAX, SMAX)))
    moved = lax.dynamic_slice_in_dim(padded, SMAX - offset, NY, 2)
    column = jnp.arange(NY, dtype=jnp.int32)
    inside = ((column >= low) & (column < high)).astype(jnp.float32)
    return moved * inside


def shards(volume, shear, footprint):
    slices = volume.shape[0]
    rows = volume.shape[1]
    bricks = lax.axis_size("depth")
    total = slices * bricks
    absorb = 2.0 / total
    flip = shear[0] > shear[total - 1]
    me = lax.axis_index("depth")
    local_shear = lax.dynamic_slice_in_dim(shear, me * slices, slices, 0)
    extended = extended_2(volume, (("depth", 0), ("tile", 1)), 1)

    def slice_step(step, acc):
        local = jnp.where(flip, slices - 1 - step, step).astype(jnp.int32)
        block = lax.dynamic_slice_in_dim(extended, local, 3, 0).astype(jnp.float32)
        cur = block[1, 1:-1]
        gz = 0.5 * (block[2, 1:-1] - block[0, 1:-1])
        gx = 0.5 * (block[1, 2:] - block[1, :-2])
        cols = jnp.pad(cur, ((0, 0), (1, 1)))
        gy = 0.5 * (cols[:, 2:] - cols[:, :-2])
        placed = colour(
            cur, gx, gy, gz, local_shear[local], footprint[0, 0], footprint[0, 1], absorb
        )
        return acc + (1.0 - acc[3:4]) * placed

    acc = lax.fori_loop(0, slices, slice_step, jnp.zeros((4, rows, NY), jnp.float32))
    partial_value = acc.astype(jnp.bfloat16)
    pieces = lax.all_to_all(partial_value[None], "depth", split_axis=3, concat_axis=0, tiled=True)

    def brick_step(position, image):
        source = jnp.where(flip, bricks - 1 - position, position).astype(jnp.int32)
        piece = lax.dynamic_index_in_dim(pieces, source, 0, keepdims=False).astype(jnp.float32)
        return image + (1.0 - image[3:4]) * piece

    start = jnp.zeros(pieces.shape[1:], jnp.float32)
    return lax.fori_loop(0, bricks, brick_step, start)


def solution(mesh):
    placed = (P("depth", "tile", None), P(), P("depth", None))
    return jax.shard_map(
        shards, mesh=mesh, in_specs=placed, out_specs=P(None, "tile", "depth"), check_vma=False
    )
```

profile of v0, /device:TPU:1, one launch (start us, length us, event | category | flops | bytes accessed | tf_op | source)
XLA Modules:
  0.0 268.8 jit_solution(5925467425739162417)
XLA Ops:
  1.3 4.0 %collective-permute-start = (bf16[1,64,4096]{2,1,0:T(8,128)(2,1)S(1)}, bf16[1,64,4096]{2,1,0:T(8,128)(2,1)S(1)}, u32[]{:S(2)}, u32[]{:S(2)}) collective-permute-start(bf16[1,64,4096]{2,1,0:T(8,128)(2,1)S(1)} %get-tuple-element.320), channel_id=1, source_target_pairs={{0,4},{4,8},{8,12},{12,16},{16,20},{20,24},{24,28},{1,5},{5,9},{9,... | collective-permute-start | bytes 1572872 | tf_op jit(solution)/shard_map/ppermute | solution.py:17
  7.3 19.7 %collective-permute-done = bf16[1,64,4096]{2,1,0:T(8,128)(2,1)S(1)} collective-permute-done((bf16[1,64,4096]{2,1,0:T(8,128)(2,1)S(1)}, bf16[1,64,4096]{2,1,0:T(8,128)(2,1)S(1)}, u32[]{:S(2)}, u32[]{:S(2)}) %collective-permute-start) | collective-permute-done | bytes 524320 | tf_op jit(solution)/shard_map/ppermute | solution.py:17
  27.1 2.5 constant_dynamic-update-slice_fusion.1
  30.0 4.6 %collective-permute-start.2 = (bf16[10,1,4096]{2,1,0:T(2,128)(2,1)S(1)}, bf16[10,1,4096]{2,1,0:T(2,128)(2,1)S(1)}, u32[]{:S(2)}, u32[]{:S(2)}) collective-permute-start(bf16[10,1,4096]{2,1,0:T(2,128)(2,1)S(1)} %get-tuple-element.317), channel_id=1, source_target_pairs={{0,1},{1,2},{2,3},{4,5},{5,6},{6,7},{8,9},{9,10},{10,11},{12,13},{... | collective-permute-start | bytes 245768 | tf_op jit(solution)/shard_map/ppermute | solution.py:17
  34.5 1.9 collective-permute-start.3
  38.3 2.9 %collective-permute-done.3 = bf16[10,1,4096]{2,1,0:T(2,128)(2,1)S(1)} collective-permute-done((bf16[10,1,4096]{2,1,0:T(2,128)(2,1)S(1)}, bf16[10,1,4096]{2,1,0:T(2,128)(2,1)S(1)}, u32[]{:S(2)}, u32[]{:S(2)}) %collective-permute-start.3) | collective-permute-done | bytes 81952 | tf_op jit(solution)/shard_map/ppermute | solution.py:18
  41.2 6.1 %pad_maximum_fusion = bf16[10,66,4096]{2,1,0:T(8,128)(2,1)} fusion(bf16[10,1,4096]{2,1,0:T(2,128)(2,1)S(1)} %collective-permute-done.3, bf16[10,64,4096]{2,1,0:T(8,128)(2,1)S(1)} %constant_dynamic-update-slice_fusion, bf16[10,1,4096]{2,1,0:T(2,128)(2,1)S(1)} %collective-permute-done.2), kind=kLoop, calls=%fused_computation.53 | loop fusion | flops 16220160 | bytes 10813440 | tf_op jit(solution)/shard_map/concatenate | solution.py:19
  47.3 135.7 %while.30 = (s32[]{:T(128)}, f32[4,64,4096]{2,1,0:T(8,128)}, pred[]{:T(512)}, bf16[10,66,4096]{2,1,0:T(8,128)(2,1)}, s32[8]{0:T(128)S(1)}, /*index=5*/s32[1,2]{1...) while((s32[]{:T(128)}, f32[4,64,4096]{2,1,0:T(8,128)}, ...), condition=%wide.region_1.2_spmd.clone, body=%wide.region_0.1_spmd.clone.sunk | while | flops 30973964 | bytes 48940876 | solution.py:66
  47.3 1.9 dynamic-slice_convert_fusion.2
  49.4 2.5 multiply_bitcast_fusion.5
  57.0 3.9 %fusion.44 = f32[4,64,4096]{2,1,0:T(8,128)} fusion(s32[]{:T(128)S(6)} %select_n.74, f32[1,64,4096]{2,1,0:T(8,128)S(1)} %get-tuple-element.391, f32[1,64,4096]{2,1,0:T(8,128)S(1)} %get-tuple-element.392, f32[1,64,4096]{2,1,0:T(8,128)S(1)} %copy-done, f32[1,64,4096]{2,1,0:T(8,128)S(1)} %get-tuple-element.394, f32[4096]{0:T(1024)S(1)} %fusion.42, ...), kind=kLoop, calls=%fused_computation.10.clone.1 | loop fusion | flops 15728640 | bytes 13649408 | tf_op jit(solution)/shard_map/while/body/eval_jaxpr/add | solution.py:64
  60.9 1.9 dynamic-slice_convert_fusion.2
  63.1 2.5 multiply_bitcast_fusion.5
  68.2 2.6 broadcast_select_fusion.4
  72.9 5.4 %fusion.44 = f32[4,64,4096]{2,1,0:T(8,128)} fusion(s32[]{:T(128)S(6)} %select_n.74, f32[1,64,4096]{2,1,0:T(8,128)S(1)} %get-tuple-element.391, f32[1,64,4096]{2,1,0:T(8,128)S(1)} %get-tuple-element.392, f32[1,64,4096]{2,1,0:T(8,128)S(1)} %copy-done, f32[1,64,4096]{2,1,0:T(8,128)S(1)} %get-tuple-element.394, f32[4096]{0:T(1024)S(1)} %fusion.42, ...), kind=kLoop, calls=%fused_computation.10.clone.1 | loop fusion | flops 15728640 | bytes 13649408 | tf_op jit(solution)/shard_map/while/body/eval_jaxpr/add | solution.py:64
  78.3 1.9 dynamic-slice_convert_fusion.2
  80.5 2.5 multiply_bitcast_fusion.5
  85.7 2.6 broadcast_select_fusion.4
  90.3 5.4 %fusion.44 = f32[4,64,4096]{2,1,0:T(8,128)} fusion(s32[]{:T(128)S(6)} %select_n.74, f32[1,64,4096]{2,1,0:T(8,128)S(1)} %get-tuple-element.391, f32[1,64,4096]{2,1,0:T(8,128)S(1)} %get-tuple-element.392, f32[1,64,4096]{2,1,0:T(8,128)S(1)} %copy-done, f32[1,64,4096]{2,1,0:T(8,128)S(1)} %get-tuple-element.394, f32[4096]{0:T(1024)S(1)} %fusion.42, ...), kind=kLoop, calls=%fused_computation.10.clone.1 | loop fusion | flops 15728640 | bytes 13649408 | tf_op jit(solution)/shard_map/while/body/eval_jaxpr/add | solution.py:64
  95.8 1.9 dynamic-slice_convert_fusion.2
  97.9 2.5 multiply_bitcast_fusion.5
  103.1 2.6 broadcast_select_fusion.4
  107.8 5.4 %fusion.44 = f32[4,64,4096]{2,1,0:T(8,128)} fusion(s32[]{:T(128)S(6)} %select_n.74, f32[1,64,4096]{2,1,0:T(8,128)S(1)} %get-tuple-element.391, f32[1,64,4096]{2,1,0:T(8,128)S(1)} %get-tuple-element.392, f32[1,64,4096]{2,1,0:T(8,128)S(1)} %copy-done, f32[1,64,4096]{2,1,0:T(8,128)S(1)} %get-tuple-element.394, f32[4096]{0:T(1024)S(1)} %fusion.42, ...), kind=kLoop, calls=%fused_computation.10.clone.1 | loop fusion | flops 15728640 | bytes 13649408 | tf_op jit(solution)/shard_map/while/body/eval_jaxpr/add | solution.py:64
  113.2 1.9 dynamic-slice_convert_fusion.2
  115.4 2.5 multiply_bitcast_fusion.5
  120.6 2.6 broadcast_select_fusion.4
  125.2 5.4 %fusion.44 = f32[4,64,4096]{2,1,0:T(8,128)} fusion(s32[]{:T(128)S(6)} %select_n.74, f32[1,64,4096]{2,1,0:T(8,128)S(1)} %get-tuple-element.391, f32[1,64,4096]{2,1,0:T(8,128)S(1)} %get-tuple-element.392, f32[1,64,4096]{2,1,0:T(8,128)S(1)} %copy-done, f32[1,64,4096]{2,1,0:T(8,128)S(1)} %get-tuple-element.394, f32[4096]{0:T(1024)S(1)} %fusion.42, ...), kind=kLoop, calls=%fused_computation.10.clone.1 | loop fusion | flops 15728640 | bytes 13649408 | tf_op jit(solution)/shard_map/while/body/eval_jaxpr/add | solution.py:64
  130.7 1.9 dynamic-slice_convert_fusion.2
  132.8 2.5 multiply_bitcast_fusion.5
  138.0 2.6 broadcast_select_fusion.4
  142.7 5.4 %fusion.44 = f32[4,64,4096]{2,1,0:T(8,128)} fusion(s32[]{:T(128)S(6)} %select_n.74, f32[1,64,4096]{2,1,0:T(8,128)S(1)} %get-tuple-element.391, f32[1,64,4096]{2,1,0:T(8,128)S(1)} %get-tuple-element.392, f32[1,64,4096]{2,1,0:T(8,128)S(1)} %copy-done, f32[1,64,4096]{2,1,0:T(8,128)S(1)} %get-tuple-element.394, f32[4096]{0:T(1024)S(1)} %fusion.42, ...), kind=kLoop, calls=%fused_computation.10.clone.1 | loop fusion | flops 15728640 | bytes 13649408 | tf_op jit(solution)/shard_map/while/body/eval_jaxpr/add | solution.py:64
  148.1 1.9 dynamic-slice_convert_fusion.2
  150.3 2.5 multiply_bitcast_fusion.5
  155.5 2.6 broadcast_select_fusion.4
  160.1 5.4 %fusion.44 = f32[4,64,4096]{2,1,0:T(8,128)} fusion(s32[]{:T(128)S(6)} %select_n.74, f32[1,64,4096]{2,1,0:T(8,128)S(1)} %get-tuple-element.391, f32[1,64,4096]{2,1,0:T(8,128)S(1)} %get-tuple-element.392, f32[1,64,4096]{2,1,0:T(8,128)S(1)} %copy-done, f32[1,64,4096]{2,1,0:T(8,128)S(1)} %get-tuple-element.394, f32[4096]{0:T(1024)S(1)} %fusion.42, ...), kind=kLoop, calls=%fused_computation.10.clone.1 | loop fusion | flops 15728640 | bytes 13649408 | tf_op jit(solution)/shard_map/while/body/eval_jaxpr/add | solution.py:64
  165.6 1.9 dynamic-slice_convert_fusion.2
  167.7 2.5 multiply_bitcast_fusion.5
  172.9 2.6 broadcast_select_fusion.4
  177.6 5.4 %fusion.44 = f32[4,64,4096]{2,1,0:T(8,128)} fusion(s32[]{:T(128)S(6)} %select_n.74, f32[1,64,4096]{2,1,0:T(8,128)S(1)} %get-tuple-element.391, f32[1,64,4096]{2,1,0:T(8,128)S(1)} %get-tuple-element.392, f32[1,64,4096]{2,1,0:T(8,128)S(1)} %copy-done, f32[1,64,4096]{2,1,0:T(8,128)S(1)} %get-tuple-element.394, f32[4096]{0:T(1024)S(1)} %fusion.42, ...), kind=kLoop, calls=%fused_computation.10.clone.1 | loop fusion | flops 15728640 | bytes 13649408 | tf_op jit(solution)/shard_map/while/body/eval_jaxpr/add | solution.py:64
  183.0 2.5 convert_element_type.52
  185.5 4.7 %copy.10 = bf16[4,64,4096]{1,0,2:T(4,128)(2,1)} copy(bf16[4,64,4096]{2,1,0:T(8,128)(2,1)S(1)} %convert_element_type.52) | data formatting | bytes 4194304
  190.2 5.3 %bitcast_bitcast_fusion = bf16[4096,1,4,64]{3,2,1,0:T(4,128)(2,1)} fusion(bf16[4,64,4096]{1,0,2:T(4,128)(2,1)} %copy.10), kind=kLoop, calls=%fused_computation.61 | loop fusion | bytes 4194304
  195.5 7.6 %reshape.29 = bf16[8,2,65536]{2,1,0:T(2,128)(2,1)} reshape(bf16[4096,1,4,64]{3,2,1,0:T(4,128)(2,1)} %bitcast_bitcast_fusion) | data formatting | bytes 4194304
  203.1 5.5 %all-to-all-start = ((bf16[8,2,65536]{2,1,0:T(2,128)(2,1)}), bf16[8,2,65536]{2,1,0:T(2,128)(2,1)S(1)}, u32[]{:S(2)}, u32[]{:S(2)}) async-start(bf16[8,2,65536]{2,1,0:T(2,128)(2,1)} %reshape.29), calls=%async_computation | async-start | bytes 4194304 | tf_op jit(solution)/shard_map/all_to_all | solution.py:68
  208.6 46.3 %all-to-all-done = bf16[8,2,65536]{2,1,0:T(2,128)(2,1)S(1)} async-done(((bf16[8,2,65536]{2,1,0:T(2,128)(2,1)}), bf16[8,2,65536]{2,1,0:T(2,128)(2,1)S(1)}, u32[]{:S(2)}, u32[]{:S(2)}) %all-to-all-start) | async-done | bytes 2097184 | tf_op jit(solution)/shard_map/all_to_all | solution.py:68
  254.9 5.0 %reshape.30 = bf16[4096,1,4,64]{3,2,1,0:T(4,128)(2,1)} reshape(bf16[8,2,65536]{2,1,0:T(2,128)(2,1)S(1)} %all-to-all-done) | data formatting | bytes 4194304
  259.9 5.6 %copy.9 = bf16[1,4,64,8,512]{4,2,1,3,0:T(8,128)(2,1)S(1)} copy(bf16[1,4,64,8,512]{2,1,4,3,0:T(4,128)(2,1)} %bitcast.87) | data formatting | bytes 4194304 | tf_op jit(solution)/shard_map/all_to_all | solution.py:68
  265.5 2.5 while.31
  (106 shorter events, 37.1 us)
Async XLA Ops:
  1.3 25.8 %collective-permute-start = (bf16[1,64,4096]{2,1,0:T(8,128)(2,1)S(1)}, bf16[1,64,4096]{2,1,0:T(8,128)(2,1)S(1)}, u32[]{:S(2)}, u32[]{:S(2)}) collective-permute-start(bf16[1,64,4096]{2,1,0:T(8,128)(2,1)S(1)} %get-tuple-element.320), channel_id=1, source_target_pairs={{0,4},{4,8},{8,12},{12,16},{16,20},{20,24},{24,28},{1,5},{5,9},{9,... | collective-permute-start | bytes 1572872 | tf_op jit(solution)/shard_map/ppermute | solution.py:17
  5.2 24.3 %collective-permute-start.1 = (bf16[1,64,4096]{2,1,0:T(8,128)(2,1)S(1)}, bf16[1,64,4096]{2,1,0:T(8,128)(2,1)S(1)}, u32[]{:S(2)}, u32[]{:S(2)}) collective-permute-start(bf16[1,64,4096]{2,1,0:T(8,128)(2,1)S(1)} %get-tuple-element.319), channel_id=1, source_target_pairs={{4,0},{8,4},{12,8},{16,12},{20,16},{24,20},{28,24},{5,1},{9,5},{13... | collective-permute-start | bytes 1572872 | tf_op jit(solution)/shard_map/ppermute | solution.py:18
  27.1 9.4 %copy-start.3 = (s32[64]{0:T(128)S(1)}, s32[64]{0:T(128)}, u32[]{:S(2)}) copy-start(s32[64]{0:T(128)} %param.8) | copy-start | bytes 772
  30.0 8.3 %collective-permute-start.2 = (bf16[10,1,4096]{2,1,0:T(2,128)(2,1)S(1)}, bf16[10,1,4096]{2,1,0:T(2,128)(2,1)S(1)}, u32[]{:S(2)}, u32[]{:S(2)}) collective-permute-start(bf16[10,1,4096]{2,1,0:T(2,128)(2,1)S(1)} %get-tuple-element.317), channel_id=1, source_target_pairs={{0,1},{1,2},{2,3},{4,5},{5,6},{6,7},{8,9},{9,10},{10,11},{12,13},{... | collective-permute-start | bytes 245768 | tf_op jit(solution)/shard_map/ppermute | solution.py:17
  34.5 6.6 %collective-permute-start.3 = (bf16[10,1,4096]{2,1,0:T(2,128)(2,1)S(1)}, bf16[10,1,4096]{2,1,0:T(2,128)(2,1)S(1)}, u32[]{:S(2)}, u32[]{:S(2)}) collective-permute-start(bf16[10,1,4096]{2,1,0:T(2,128)(2,1)S(1)} %get-tuple-element.318), channel_id=1, source_target_pairs={{1,0},{2,1},{3,2},{5,4},{6,5},{7,6},{9,8},{10,9},{11,10},{13,12},{... | collective-permute-start | bytes 245768 | tf_op jit(solution)/shard_map/ppermute | solution.py:18
  38.3 9.0 %copy-start.2 = (s32[1,2]{1,0:T(1,128)S(1)}, s32[1,2]{1,0:T(1,128)}, u32[]{:S(2)}) copy-start(s32[1,2]{1,0:T(1,128)} %param.9) | copy-start | bytes 28
  54.6 2.4 copy-start
  68.2 4.7 %copy-start = (f32[1,64,4096]{2,1,0:T(8,128)S(1)}, f32[1,64,4096]{2,1,0:T(8,128)}, u32[]{:S(2)}) copy-start(f32[1,64,4096]{2,1,0:T(8,128)} %get-tuple-element.393) | copy-start | bytes 3145732 | tf_op jit(solution)/shard_map/while
  85.7 4.7 %copy-start = (f32[1,64,4096]{2,1,0:T(8,128)S(1)}, f32[1,64,4096]{2,1,0:T(8,128)}, u32[]{:S(2)}) copy-start(f32[1,64,4096]{2,1,0:T(8,128)} %get-tuple-element.393) | copy-start | bytes 3145732 | tf_op jit(solution)/shard_map/while
  103.1 4.7 %copy-start = (f32[1,64,4096]{2,1,0:T(8,128)S(1)}, f32[1,64,4096]{2,1,0:T(8,128)}, u32[]{:S(2)}) copy-start(f32[1,64,4096]{2,1,0:T(8,128)} %get-tuple-element.393) | copy-start | bytes 3145732 | tf_op jit(solution)/shard_map/while
  120.6 4.7 %copy-start = (f32[1,64,4096]{2,1,0:T(8,128)S(1)}, f32[1,64,4096]{2,1,0:T(8,128)}, u32[]{:S(2)}) copy-start(f32[1,64,4096]{2,1,0:T(8,128)} %get-tuple-element.393) | copy-start | bytes 3145732 | tf_op jit(solution)/shard_map/while
  138.0 4.7 %copy-start = (f32[1,64,4096]{2,1,0:T(8,128)S(1)}, f32[1,64,4096]{2,1,0:T(8,128)}, u32[]{:S(2)}) copy-start(f32[1,64,4096]{2,1,0:T(8,128)} %get-tuple-element.393) | copy-start | bytes 3145732 | tf_op jit(solution)/shard_map/while
  155.4 4.7 %copy-start = (f32[1,64,4096]{2,1,0:T(8,128)S(1)}, f32[1,64,4096]{2,1,0:T(8,128)}, u32[]{:S(2)}) copy-start(f32[1,64,4096]{2,1,0:T(8,128)} %get-tuple-element.393) | copy-start | bytes 3145732 | tf_op jit(solution)/shard_map/while
  172.9 4.7 %copy-start = (f32[1,64,4096]{2,1,0:T(8,128)S(1)}, f32[1,64,4096]{2,1,0:T(8,128)}, u32[]{:S(2)}) copy-start(f32[1,64,4096]{2,1,0:T(8,128)} %get-tuple-element.393) | copy-start | bytes 3145732 | tf_op jit(solution)/shard_map/while
  203.1 51.8 %all-to-all-start = ((bf16[8,2,65536]{2,1,0:T(2,128)(2,1)}), bf16[8,2,65536]{2,1,0:T(2,128)(2,1)S(1)}, u32[]{:S(2)}, u32[]{:S(2)}) async-start(bf16[8,2,65536]{2,1,0:T(2,128)(2,1)} %reshape.29), calls=%async_computation | async-start | bytes 4194304 | tf_op jit(solution)/shard_map/all_to_all | solution.py:68
  268.0 0.8 copy-start.1
where the time goes:
time: 270 us; the launch traced here: 269 us
  other arithmetic  125 us (46%)
  waiting for transfers between devices  69 us (26%)
  local copies, waits for them, and re-layouts  44.4 us (16%)
  starting transfers between devices  17.2 us (6%)
  loops' own time  11.3 us (4%)
    all_to_all x1, waiting for transfers between devices, shards(): lax.all_to_all(partial_value[None], 'depth', split_axis=3, concat_axis=0,...  46.3 us
    add x8, other arithmetic, slice_step(): return acc + (1.0 - acc[3:4]) * placed  41.9 us
    another operation x16, other arithmetic, colour(): jnp.stack([shade * jax.nn.sigmoid(1.2 * cur + 0.2) * alpha, shade * jax.n...  26.2 us
    unnamed x12, local copies, waits for them, and re-layouts  25.9 us
    ppermute x2, waiting for transfers between devices, extended_2(): before = lax.ppermute(last, axis, up)  19.7 us
    while x16, other arithmetic  18.5 us
    convert_element_type x8, other arithmetic, slice_step(): block = lax.dynamic_slice_in_dim(extended, local, 3, 0).astype(jnp.float32)  15 us
    another operation x1, loops' own time, shards(): lax.fori_loop(0, slices, slice_step, jnp.zeros((4, rows, NY), jnp.float32))  11 us
  transfers between devices with their start and end apart: 5, of which 3 were waited for; matrix products, arithmetic and copies ran while one was open for 1% of the time, Pallas kernels for 0%

commit v1 on v0

--- a/solution.py
+++ b/solution.py
@@ -65,7 +65,12 @@
 
     acc = lax.fori_loop(0, slices, slice_step, jnp.zeros((4, rows, NY), jnp.float32))
     partial_value = acc.astype(jnp.bfloat16)
-    pieces = lax.all_to_all(partial_value[None], "depth", split_axis=3, concat_axis=0, tiled=True)
+    pieces = jnp.concatenate(
+        lax.all_to_all(
+            jnp.stack(jnp.split(partial_value[None], lax.axis_size("depth"), axis=3)), "depth", 0, 0
+        ),
+        axis=0,
+    )
 
     def brick_step(position, image):
         source = jnp.where(flip, bricks - 1 - position, position).astype(jnp.int32)

time: 270 us -> 247 us (0.915)
  local copies, waits for them, and re-layouts: 44.4 us -> 22 us
    unnamed x12 -> x15, local copies, waits for them, and re-layouts: 25.9 us -> 8.33 us
    all_to_all x1 -> x0, local copies, waits for them, and re-layouts: 5.58 us -> none  [shards(): lax.all_to_all(partial_value[None], 'depth', split_axis=3, concat_axis=0,...]
  transfers between devices with their start and end apart: 5 -> 5, of which waited for: 3 -> 3; matrix products, arithmetic and copies ran while one was open for 1% -> 2% of each run, Pallas kernels for 0% -> 0%
where the time goes in v1:
time: 247 us; the launch traced here: 246 us
  other arithmetic  125 us (51%)
  waiting for transfers between devices  69 us (28%)
  local copies, waits for them, and re-layouts  22 us (9%)
  starting transfers between devices  17.2 us (7%)
  loops' own time  11.3 us (5%)
    all_to_all x1, waiting for transfers between devices, shards(): lax.all_to_all(jnp.stack(jnp.split(partial_value[None], lax.axis_size('de...  46.3 us
    add x8, other arithmetic, slice_step(): return acc + (1.0 - acc[3:4]) * placed  41.9 us
    another operation x16, other arithmetic, colour(): jnp.stack([shade * jax.nn.sigmoid(1.2 * cur + 0.2) * alpha, shade * jax.n...  26.2 us
    ppermute x2, waiting for transfers between devices, extended_2(): before = lax.ppermute(last, axis, up)  19.7 us
    while x16, other arithmetic  18.5 us
    convert_element_type x8, other arithmetic, slice_step(): block = lax.dynamic_slice_in_dim(extended, local, 3, 0).astype(jnp.float32)  15 us
    another operation x1, loops' own time, shards(): lax.fori_loop(0, slices, slice_step, jnp.zeros((4, rows, NY), jnp.float32))  11 us
    convert_element_type x8, other arithmetic, colour(): inside = ((column >= low) & (column < high)).astype(jnp.float32)  10.7 us
  transfers between devices with their start and end apart: 5, of which 3 were waited for; matrix products, arithmetic and copies ran while one was open for 2% of the time, Pallas kernels for 0%

profile of v1, /device:TPU:1, one launch (start us, length us, event | category | flops | bytes accessed | tf_op | source)
XLA Modules:
  0.0 246.4 jit_solution(7275596192450826629)
XLA Ops:
  1.3 4.0 %collective-permute-start = (bf16[1,64,4096]{2,1,0:T(8,128)(2,1)S(1)}, bf16[1,64,4096]{2,1,0:T(8,128)(2,1)S(1)}, u32[]{:S(2)}, u32[]{:S(2)}) collective-permute-start(bf16[1,64,4096]{2,1,0:T(8,128)(2,1)S(1)} %get-tuple-element.312), channel_id=1, source_target_pairs={{0,4},{4,8},{8,12},{12,16},{16,20},{20,24},{24,28},{1,5},{5,9},{9,... | collective-permute-start | bytes 1572872 | tf_op jit(solution)/shard_map/ppermute | solution.py:17
  7.3 19.7 %collective-permute-done = bf16[1,64,4096]{2,1,0:T(8,128)(2,1)S(1)} collective-permute-done((bf16[1,64,4096]{2,1,0:T(8,128)(2,1)S(1)}, bf16[1,64,4096]{2,1,0:T(8,128)(2,1)S(1)}, u32[]{:S(2)}, u32[]{:S(2)}) %collective-permute-start) | collective-permute-done | bytes 524320 | tf_op jit(solution)/shard_map/ppermute | solution.py:17
  27.1 2.5 %constant_dynamic-update-slice_fusion.1 = bf16[10,64,4096]{2,1,0:T(8,128)(2,1)S(1)} fusion(bf16[10,64,4096]{2,1,0:T(8,128)(2,1)S(1)} %constant_dynamic-update-slice_fusion.2, bf16[8,64,4096]{2,1,0:T(8,128)(2,1)} %param.7), kind=kLoop, calls=%fused_computation.72 | loop fusion | bytes 8388608
  30.0 4.6 %collective-permute-start.2 = (bf16[10,1,4096]{2,1,0:T(2,128)(2,1)S(1)}, bf16[10,1,4096]{2,1,0:T(2,128)(2,1)S(1)}, u32[]{:S(2)}, u32[]{:S(2)}) collective-permute-start(bf16[10,1,4096]{2,1,0:T(2,128)(2,1)S(1)} %get-tuple-element.309), channel_id=1, source_target_pairs={{0,1},{1,2},{2,3},{4,5},{5,6},{6,7},{8,9},{9,10},{10,11},{12,13},{... | collective-permute-start | bytes 245768 | tf_op jit(solution)/shard_map/ppermute | solution.py:17
  34.5 1.9 collective-permute-start.3
  38.3 2.9 %collective-permute-done.3 = bf16[10,1,4096]{2,1,0:T(2,128)(2,1)S(1)} collective-permute-done((bf16[10,1,4096]{2,1,0:T(2,128)(2,1)S(1)}, bf16[10,1,4096]{2,1,0:T(2,128)(2,1)S(1)}, u32[]{:S(2)}, u32[]{:S(2)}) %collective-permute-start.3) | collective-permute-done | bytes 81952 | tf_op jit(solution)/shard_map/ppermute | solution.py:18
  41.2 6.1 %pad_maximum_fusion = bf16[10,66,4096]{2,1,0:T(8,128)(2,1)} fusion(bf16[10,1,4096]{2,1,0:T(2,128)(2,1)S(1)} %collective-permute-done.3, bf16[10,64,4096]{2,1,0:T(8,128)(2,1)S(1)} %constant_dynamic-update-slice_fusion, bf16[10,1,4096]{2,1,0:T(2,128)(2,1)S(1)} %collective-permute-done.2), kind=kLoop, calls=%fused_computation.53 | loop fusion | flops 16220160 | bytes 10813440 | tf_op jit(solution)/shard_map/concatenate | solution.py:19
  47.3 135.7 %while.30 = (s32[]{:T(128)}, f32[4,64,4096]{2,1,0:T(8,128)}, pred[]{:T(512)}, bf16[10,66,4096]{2,1,0:T(8,128)(2,1)}, s32[8]{0:T(128)S(1)}, /*index=5*/s32[1,2]{1...) while((s32[]{:T(128)}, f32[4,64,4096]{2,1,0:T(8,128)}, ...), condition=%wide.region_1.2_spmd.clone, body=%wide.region_0.1_spmd.clone.sunk | while | flops 30973964 | bytes 48940876 | solution.py:66
  47.3 1.9 dynamic-slice_convert_fusion.2
  49.4 2.5 %multiply_bitcast_fusion.5 = (f32[1,64,4096]{2,1,0:T(8,128)}, f32[64,4096]{1,0:T(8,128)S(1)}) fusion(f32[3,66,4096]{2,1,0:T(8,128)S(1)} %dynamic-slice_convert_fusion.2, f32[64,4096]{1,0:T(8,128)S(1)} %get-tuple-element.381), kind=kLoop, calls=%fused_computation.40.clone.1 | loop fusion | flops 8126464 | bytes 8388608 | tf_op jit(solution)/shard_map/while/body/eval_jaxpr/stack | solution.py:27
  55.7 1.3 fusion.50
  57.0 3.9 %fusion.52 = f32[4,64,4096]{2,1,0:T(8,128)} fusion(s32[]{:T(128)S(6)} %select_n.74, f32[1,64,4096]{2,1,0:T(8,128)S(1)} %get-tuple-element.383, f32[1,64,4096]{2,1,0:T(8,128)S(1)} %get-tuple-element.384, f32[1,64,4096]{2,1,0:T(8,128)S(1)} %copy-done, f32[1,64,4096]{2,1,0:T(8,128)S(1)} %get-tuple-element.386, f32[4096]{0:T(1024)S(1)} %fusion.50, ...), kind=kLoop, calls=%fused_computation.10.clone.1 | loop fusion | flops 15728640 | bytes 13649408 | tf_op jit(solution)/shard_map/while/body/eval_jaxpr/add | solution.py:64
  60.9 1.9 dynamic-slice_convert_fusion.2
  63.1 2.5 %multiply_bitcast_fusion.5 = (f32[1,64,4096]{2,1,0:T(8,128)}, f32[64,4096]{1,0:T(8,128)S(1)}) fusion(f32[3,66,4096]{2,1,0:T(8,128)S(1)} %dynamic-slice_convert_fusion.2, f32[64,4096]{1,0:T(8,128)S(1)} %get-tuple-element.381), kind=kLoop, calls=%fused_computation.40.clone.1 | loop fusion | flops 8126464 | bytes 8388608 | tf_op jit(solution)/shard_map/while/body/eval_jaxpr/stack | solution.py:27
  68.2 2.6 %broadcast_select_fusion.4 = f32[4,64,4096]{2,1,0:T(8,128)S(1)} fusion(f32[4,64,4096]{2,1,0:T(8,128)} %get-tuple-element.407, pred[]{:T(512)S(6)} %compare.28), kind=kLoop, calls=%fused_computation.18.clone.2 | loop fusion | flops 1048576 | bytes 8388609 | tf_op jit(solution)/shard_map/while
  71.5 1.3 fusion.50
  72.9 5.4 %fusion.52 = f32[4,64,4096]{2,1,0:T(8,128)} fusion(s32[]{:T(128)S(6)} %select_n.74, f32[1,64,4096]{2,1,0:T(8,128)S(1)} %get-tuple-element.383, f32[1,64,4096]{2,1,0:T(8,128)S(1)} %get-tuple-element.384, f32[1,64,4096]{2,1,0:T(8,128)S(1)} %copy-done, f32[1,64,4096]{2,1,0:T(8,128)S(1)} %get-tuple-element.386, f32[4096]{0:T(1024)S(1)} %fusion.50, ...), kind=kLoop, calls=%fused_computation.10.clone.1 | loop fusion | flops 15728640 | bytes 13649408 | tf_op jit(solution)/shard_map/while/body/eval_jaxpr/add | solution.py:64
  78.3 1.9 dynamic-slice_convert_fusion.2
  80.5 2.5 %multiply_bitcast_fusion.5 = (f32[1,64,4096]{2,1,0:T(8,128)}, f32[64,4096]{1,0:T(8,128)S(1)}) fusion(f32[3,66,4096]{2,1,0:T(8,128)S(1)} %dynamic-slice_convert_fusion.2, f32[64,4096]{1,0:T(8,128)S(1)} %get-tuple-element.381), kind=kLoop, calls=%fused_computation.40.clone.1 | loop fusion | flops 8126464 | bytes 8388608 | tf_op jit(solution)/shard_map/while/body/eval_jaxpr/stack | solution.py:27
  85.7 2.6 %broadcast_select_fusion.4 = f32[4,64,4096]{2,1,0:T(8,128)S(1)} fusion(f32[4,64,4096]{2,1,0:T(8,128)} %get-tuple-element.407, pred[]{:T(512)S(6)} %compare.28), kind=kLoop, calls=%fused_computation.18.clone.2 | loop fusion | flops 1048576 | bytes 8388609 | tf_op jit(solution)/shard_map/while
  89.0 1.3 fusion.50
  90.3 5.4 %fusion.52 = f32[4,64,4096]{2,1,0:T(8,128)} fusion(s32[]{:T(128)S(6)} %select_n.74, f32[1,64,4096]{2,1,0:T(8,128)S(1)} %get-tuple-element.383, f32[1,64,4096]{2,1,0:T(8,128)S(1)} %get-tuple-element.384, f32[1,64,4096]{2,1,0:T(8,128)S(1)} %copy-done, f32[1,64,4096]{2,1,0:T(8,128)S(1)} %get-tuple-element.386, f32[4096]{0:T(1024)S(1)} %fusion.50, ...), kind=kLoop, calls=%fused_computation.10.clone.1 | loop fusion | flops 15728640 | bytes 13649408 | tf_op jit(solution)/shard_map/while/body/eval_jaxpr/add | solution.py:64
  95.8 1.9 dynamic-slice_convert_fusion.2
  97.9 2.5 %multiply_bitcast_fusion.5 = (f32[1,64,4096]{2,1,0:T(8,128)}, f32[64,4096]{1,0:T(8,128)S(1)}) fusion(f32[3,66,4096]{2,1,0:T(8,128)S(1)} %dynamic-slice_convert_fusion.2, f32[64,4096]{1,0:T(8,128)S(1)} %get-tuple-element.381), kind=kLoop, calls=%fused_computation.40.clone.1 | loop fusion | flops 8126464 | bytes 8388608 | tf_op jit(solution)/shard_map/while/body/eval_jaxpr/stack | solution.py:27
  103.1 2.6 %broadcast_select_fusion.4 = f32[4,64,4096]{2,1,0:T(8,128)S(1)} fusion(f32[4,64,4096]{2,1,0:T(8,128)} %get-tuple-element.407, pred[]{:T(512)S(6)} %compare.28), kind=kLoop, calls=%fused_computation.18.clone.2 | loop fusion | flops 1048576 | bytes 8388609 | tf_op jit(solution)/shard_map/while
  107.8 5.4 %fusion.52 = f32[4,64,4096]{2,1,0:T(8,128)} fusion(s32[]{:T(128)S(6)} %select_n.74, f32[1,64,4096]{2,1,0:T(8,128)S(1)} %get-tuple-element.383, f32[1,64,4096]{2,1,0:T(8,128)S(1)} %get-tuple-element.384, f32[1,64,4096]{2,1,0:T(8,128)S(1)} %copy-done, f32[1,64,4096]{2,1,0:T(8,128)S(1)} %get-tuple-element.386, f32[4096]{0:T(1024)S(1)} %fusion.50, ...), kind=kLoop, calls=%fused_computation.10.clone.1 | loop fusion | flops 15728640 | bytes 13649408 | tf_op jit(solution)/shard_map/while/body/eval_jaxpr/add | solution.py:64
  113.2 1.9 dynamic-slice_convert_fusion.2
  115.4 2.5 %multiply_bitcast_fusion.5 = (f32[1,64,4096]{2,1,0:T(8,128)}, f32[64,4096]{1,0:T(8,128)S(1)}) fusion(f32[3,66,4096]{2,1,0:T(8,128)S(1)} %dynamic-slice_convert_fusion.2, f32[64,4096]{1,0:T(8,128)S(1)} %get-tuple-element.381), kind=kLoop, calls=%fused_computation.40.clone.1 | loop fusion | flops 8126464 | bytes 8388608 | tf_op jit(solution)/shard_map/while/body/eval_jaxpr/stack | solution.py:27
  120.6 2.6 %broadcast_select_fusion.4 = f32[4,64,4096]{2,1,0:T(8,128)S(1)} fusion(f32[4,64,4096]{2,1,0:T(8,128)} %get-tuple-element.407, pred[]{:T(512)S(6)} %compare.28), kind=kLoop, calls=%fused_computation.18.clone.2 | loop fusion | flops 1048576 | bytes 8388609 | tf_op jit(solution)/shard_map/while
  123.9 1.3 fusion.50
  125.2 5.4 %fusion.52 = f32[4,64,4096]{2,1,0:T(8,128)} fusion(s32[]{:T(128)S(6)} %select_n.74, f32[1,64,4096]{2,1,0:T(8,128)S(1)} %get-tuple-element.383, f32[1,64,4096]{2,1,0:T(8,128)S(1)} %get-tuple-element.384, f32[1,64,4096]{2,1,0:T(8,128)S(1)} %copy-done, f32[1,64,4096]{2,1,0:T(8,128)S(1)} %get-tuple-element.386, f32[4096]{0:T(1024)S(1)} %fusion.50, ...), kind=kLoop, calls=%fused_computation.10.clone.1 | loop fusion | flops 15728640 | bytes 13649408 | tf_op jit(solution)/shard_map/while/body/eval_jaxpr/add | solution.py:64
  130.7 1.9 dynamic-slice_convert_fusion.2
  132.8 2.5 %multiply_bitcast_fusion.5 = (f32[1,64,4096]{2,1,0:T(8,128)}, f32[64,4096]{1,0:T(8,128)S(1)}) fusion(f32[3,66,4096]{2,1,0:T(8,128)S(1)} %dynamic-slice_convert_fusion.2, f32[64,4096]{1,0:T(8,128)S(1)} %get-tuple-element.381), kind=kLoop, calls=%fused_computation.40.clone.1 | loop fusion | flops 8126464 | bytes 8388608 | tf_op jit(solution)/shard_map/while/body/eval_jaxpr/stack | solution.py:27
  138.0 2.6 %broadcast_select_fusion.4 = f32[4,64,4096]{2,1,0:T(8,128)S(1)} fusion(f32[4,64,4096]{2,1,0:T(8,128)} %get-tuple-element.407, pred[]{:T(512)S(6)} %compare.28), kind=kLoop, calls=%fused_computation.18.clone.2 | loop fusion | flops 1048576 | bytes 8388609 | tf_op jit(solution)/shard_map/while
  141.3 1.3 fusion.50
  142.7 5.4 %fusion.52 = f32[4,64,4096]{2,1,0:T(8,128)} fusion(s32[]{:T(128)S(6)} %select_n.74, f32[1,64,4096]{2,1,0:T(8,128)S(1)} %get-tuple-element.383, f32[1,64,4096]{2,1,0:T(8,128)S(1)} %get-tuple-element.384, f32[1,64,4096]{2,1,0:T(8,128)S(1)} %copy-done, f32[1,64,4096]{2,1,0:T(8,128)S(1)} %get-tuple-element.386, f32[4096]{0:T(1024)S(1)} %fusion.50, ...), kind=kLoop, calls=%fused_computation.10.clone.1 | loop fusion | flops 15728640 | bytes 13649408 | tf_op jit(solution)/shard_map/while/body/eval_jaxpr/add | solution.py:64
  148.1 1.9 dynamic-slice_convert_fusion.2
  150.3 2.5 %multiply_bitcast_fusion.5 = (f32[1,64,4096]{2,1,0:T(8,128)}, f32[64,4096]{1,0:T(8,128)S(1)}) fusion(f32[3,66,4096]{2,1,0:T(8,128)S(1)} %dynamic-slice_convert_fusion.2, f32[64,4096]{1,0:T(8,128)S(1)} %get-tuple-element.381), kind=kLoop, calls=%fused_computation.40.clone.1 | loop fusion | flops 8126464 | bytes 8388608 | tf_op jit(solution)/shard_map/while/body/eval_jaxpr/stack | solution.py:27
  155.5 2.6 %broadcast_select_fusion.4 = f32[4,64,4096]{2,1,0:T(8,128)S(1)} fusion(f32[4,64,4096]{2,1,0:T(8,128)} %get-tuple-element.407, pred[]{:T(512)S(6)} %compare.28), kind=kLoop, calls=%fused_computation.18.clone.2 | loop fusion | flops 1048576 | bytes 8388609 | tf_op jit(solution)/shard_map/while
  160.1 5.4 %fusion.52 = f32[4,64,4096]{2,1,0:T(8,128)} fusion(s32[]{:T(128)S(6)} %select_n.74, f32[1,64,4096]{2,1,0:T(8,128)S(1)} %get-tuple-element.383, f32[1,64,4096]{2,1,0:T(8,128)S(1)} %get-tuple-element.384, f32[1,64,4096]{2,1,0:T(8,128)S(1)} %copy-done, f32[1,64,4096]{2,1,0:T(8,128)S(1)} %get-tuple-element.386, f32[4096]{0:T(1024)S(1)} %fusion.50, ...), kind=kLoop, calls=%fused_computation.10.clone.1 | loop fusion | flops 15728640 | bytes 13649408 | tf_op jit(solution)/shard_map/while/body/eval_jaxpr/add | solution.py:64
  165.6 1.9 dynamic-slice_convert_fusion.2
  167.7 2.5 %multiply_bitcast_fusion.5 = (f32[1,64,4096]{2,1,0:T(8,128)}, f32[64,4096]{1,0:T(8,128)S(1)}) fusion(f32[3,66,4096]{2,1,0:T(8,128)S(1)} %dynamic-slice_convert_fusion.2, f32[64,4096]{1,0:T(8,128)S(1)} %get-tuple-element.381), kind=kLoop, calls=%fused_computation.40.clone.1 | loop fusion | flops 8126464 | bytes 8388608 | tf_op jit(solution)/shard_map/while/body/eval_jaxpr/stack | solution.py:27
  172.9 2.6 %broadcast_select_fusion.4 = f32[4,64,4096]{2,1,0:T(8,128)S(1)} fusion(f32[4,64,4096]{2,1,0:T(8,128)} %get-tuple-element.407, pred[]{:T(512)S(6)} %compare.28), kind=kLoop, calls=%fused_computation.18.clone.2 | loop fusion | flops 1048576 | bytes 8388609 | tf_op jit(solution)/shard_map/while
  177.6 5.4 %fusion.52 = f32[4,64,4096]{2,1,0:T(8,128)} fusion(s32[]{:T(128)S(6)} %select_n.74, f32[1,64,4096]{2,1,0:T(8,128)S(1)} %get-tuple-element.383, f32[1,64,4096]{2,1,0:T(8,128)S(1)} %get-tuple-element.384, f32[1,64,4096]{2,1,0:T(8,128)S(1)} %copy-done, f32[1,64,4096]{2,1,0:T(8,128)S(1)} %get-tuple-element.386, f32[4096]{0:T(1024)S(1)} %fusion.50, ...), kind=kLoop, calls=%fused_computation.10.clone.1 | loop fusion | flops 15728640 | bytes 13649408 | tf_op jit(solution)/shard_map/while/body/eval_jaxpr/add | solution.py:64
  183.0 2.5 convert_bitcast_fusion
  191.2 5.5 %all-to-all-start = ((bf16[8,1,4,64,512]{4,3,2,1,0:T(8,128)(2,1)}), bf16[8,1,4,64,512]{4,3,2,1,0:T(8,128)(2,1)S(1)}, u32[]{:S(2)}, u32[]{:S(2)}) async-start(bf16[8,1,4,64,512]{4,3,2,1,0:T(8,128)(2,1)} %fusion.28), calls=%async_computation | async-start | bytes 4194304 | tf_op jit(solution)/shard_map/all_to_all | solution.py:69
  196.7 46.3 %all-to-all-done = bf16[8,1,4,64,512]{4,3,2,1,0:T(8,128)(2,1)S(1)} async-done(((bf16[8,1,4,64,512]{4,3,2,1,0:T(8,128)(2,1)}), bf16[8,1,4,64,512]{4,3,2,1,0:T(8,128)(2,1)S(1)}, u32[]{:S(2)}, u32[]{:S(2)}) %all-to-all-start) | async-done | bytes 2097184 | tf_op jit(solution)/shard_map/all_to_all | solution.py:69
  243.1 2.5 %while.31 = (s32[]{:T(128)}, f32[4,64,512]{2,1,0:T(8,128)S(1)}, pred[]{:T(512)}, bf16[8,4,64,512]{3,2,1,0:T(8,128)(2,1)S(1)}, s32[]{:T(128)}, /*index=5*/s32[]{:T(128)}, s32[]{:T(128)}, s32[]{:T(128)}) while((s32[]{:T(128)}, f32[4,64,512]{2,1,0:T(8,128)S(1)}, pred[]{:T(512)}, bf16[8,4,64,512]{3,2,1,0:T(8,128)(2,1)S(1)}, s32[]{:T(128)}, ...), condition=%wide.region_3.4_spmd.clone, body=%wide.region_2.3_spmd.clone.sunk | while | flops 688136 | bytes 2752671 | solution.py:81
  (109 shorter events, 36.2 us)
Async XLA Ops:
  1.3 25.8 %collective-permute-start = (bf16[1,64,4096]{2,1,0:T(8,128)(2,1)S(1)}, bf16[1,64,4096]{2,1,0:T(8,128)(2,1)S(1)}, u32[]{:S(2)}, u32[]{:S(2)}) collective-permute-start(bf16[1,64,4096]{2,1,0:T(8,128)(2,1)S(1)} %get-tuple-element.312), channel_id=1, source_target_pairs={{0,4},{4,8},{8,12},{12,16},{16,20},{20,24},{24,28},{1,5},{5,9},{9,... | collective-permute-start | bytes 1572872 | tf_op jit(solution)/shard_map/ppermute | solution.py:17
  5.2 24.3 %collective-permute-start.1 = (bf16[1,64,4096]{2,1,0:T(8,128)(2,1)S(1)}, bf16[1,64,4096]{2,1,0:T(8,128)(2,1)S(1)}, u32[]{:S(2)}, u32[]{:S(2)}) collective-permute-start(bf16[1,64,4096]{2,1,0:T(8,128)(2,1)S(1)} %get-tuple-element.311), channel_id=1, source_target_pairs={{4,0},{8,4},{12,8},{16,12},{20,16},{24,20},{28,24},{5,1},{9,5},{13... | collective-permute-start | bytes 1572872 | tf_op jit(solution)/shard_map/ppermute | solution.py:18
  27.1 9.4 %copy-start.3 = (s32[64]{0:T(128)S(1)}, s32[64]{0:T(128)}, u32[]{:S(2)}) copy-start(s32[64]{0:T(128)} %param.8) | copy-start | bytes 772
  30.0 8.3 %collective-permute-start.2 = (bf16[10,1,4096]{2,1,0:T(2,128)(2,1)S(1)}, bf16[10,1,4096]{2,1,0:T(2,128)(2,1)S(1)}, u32[]{:S(2)}, u32[]{:S(2)}) collective-permute-start(bf16[10,1,4096]{2,1,0:T(2,128)(2,1)S(1)} %get-tuple-element.309), channel_id=1, source_target_pairs={{0,1},{1,2},{2,3},{4,5},{5,6},{6,7},{8,9},{9,10},{10,11},{12,13},{... | collective-permute-start | bytes 245768 | tf_op jit(solution)/shard_map/ppermute | solution.py:17
  34.5 6.6 %collective-permute-start.3 = (bf16[10,1,4096]{2,1,0:T(2,128)(2,1)S(1)}, bf16[10,1,4096]{2,1,0:T(2,128)(2,1)S(1)}, u32[]{:S(2)}, u32[]{:S(2)}) collective-permute-start(bf16[10,1,4096]{2,1,0:T(2,128)(2,1)S(1)} %get-tuple-element.310), channel_id=1, source_target_pairs={{1,0},{2,1},{3,2},{5,4},{6,5},{7,6},{9,8},{10,9},{11,10},{13,12},{... | collective-permute-start | bytes 245768 | tf_op jit(solution)/shard_map/ppermute | solution.py:18
  38.3 9.0 %copy-start.2 = (s32[1,2]{1,0:T(1,128)S(1)}, s32[1,2]{1,0:T(1,128)}, u32[]{:S(2)}) copy-start(s32[1,2]{1,0:T(1,128)} %param.9) | copy-start | bytes 28
  54.6 2.4 copy-start
  68.2 4.7 %copy-start = (f32[1,64,4096]{2,1,0:T(8,128)S(1)}, f32[1,64,4096]{2,1,0:T(8,128)}, u32[]{:S(2)}) copy-start(f32[1,64,4096]{2,1,0:T(8,128)} %get-tuple-element.385) | copy-start | bytes 3145732 | tf_op jit(solution)/shard_map/while
  85.7 4.7 %copy-start = (f32[1,64,4096]{2,1,0:T(8,128)S(1)}, f32[1,64,4096]{2,1,0:T(8,128)}, u32[]{:S(2)}) copy-start(f32[1,64,4096]{2,1,0:T(8,128)} %get-tuple-element.385) | copy-start | bytes 3145732 | tf_op jit(solution)/shard_map/while
  103.1 4.7 %copy-start = (f32[1,64,4096]{2,1,0:T(8,128)S(1)}, f32[1,64,4096]{2,1,0:T(8,128)}, u32[]{:S(2)}) copy-start(f32[1,64,4096]{2,1,0:T(8,128)} %get-tuple-element.385) | copy-start | bytes 3145732 | tf_op jit(solution)/shard_map/while
  120.6 4.7 %copy-start = (f32[1,64,4096]{2,1,0:T(8,128)S(1)}, f32[1,64,4096]{2,1,0:T(8,128)}, u32[]{:S(2)}) copy-start(f32[1,64,4096]{2,1,0:T(8,128)} %get-tuple-element.385) | copy-start | bytes 3145732 | tf_op jit(solution)/shard_map/while
  138.0 4.7 %copy-start = (f32[1,64,4096]{2,1,0:T(8,128)S(1)}, f32[1,64,4096]{2,1,0:T(8,128)}, u32[]{:S(2)}) copy-start(f32[1,64,4096]{2,1,0:T(8,128)} %get-tuple-element.385) | copy-start | bytes 3145732 | tf_op jit(solution)/shard_map/while
  155.4 4.7 %copy-start = (f32[1,64,4096]{2,1,0:T(8,128)S(1)}, f32[1,64,4096]{2,1,0:T(8,128)}, u32[]{:S(2)}) copy-start(f32[1,64,4096]{2,1,0:T(8,128)} %get-tuple-element.385) | copy-start | bytes 3145732 | tf_op jit(solution)/shard_map/while
  172.9 4.7 %copy-start = (f32[1,64,4096]{2,1,0:T(8,128)S(1)}, f32[1,64,4096]{2,1,0:T(8,128)}, u32[]{:S(2)}) copy-start(f32[1,64,4096]{2,1,0:T(8,128)} %get-tuple-element.385) | copy-start | bytes 3145732 | tf_op jit(solution)/shard_map/while
  191.2 51.8 %all-to-all-start = ((bf16[8,1,4,64,512]{4,3,2,1,0:T(8,128)(2,1)}), bf16[8,1,4,64,512]{4,3,2,1,0:T(8,128)(2,1)S(1)}, u32[]{:S(2)}, u32[]{:S(2)}) async-start(bf16[8,1,4,64,512]{4,3,2,1,0:T(8,128)(2,1)} %fusion.28), calls=%async_computation | async-start | bytes 4194304 | tf_op jit(solution)/shard_map/all_to_all | solution.py:69
  245.6 0.8 copy-start.1
